TPU v7x, 32 devices: a whole 2x2x4 slice. The times are simulated.
32 devices in a mesh: gx: 8 (over z, y), gy: 4 (over x, core).
Axes of the slice: x: 2, y: 2, z: 4, core: 2. Of those that a mesh axis runs over, the one named last changes fastest.
Arguments:
- anomalies: float32 [80, 16, 32, 128], P(None, 'gx', 'gy'), may hold values from -6 to 6
- state_mean: float32 [16, 32, 128], P('gx', 'gy'), may hold values from -6 to 6
- obs_value: float32 [16, 256], P(None, 'gy'), may hold values from -8 to 8
- obs_cell: int32 [16, 256], replicated, may hold values from 0 to 2047
- owner: int32 [16], replicated, may hold values from 0 to 7, as said below
- order: int32 [16], replicated, may hold values from 0 to 15, each once
- root_inv: float32 [16, 256, 256], P(None, 'gy'), as said below
- gain_inv: float32 [16, 256, 256], P(None, 'gy'), as said below
Outputs:
- post_anomalies: float32 [80, 16, 32, 128], P(None, 'gx', 'gy')
- post_mean: float32 [16, 32, 128], P('gx', 'gy')
Inputs may be any that keep to these rules, and one draw needn't show every extreme that they name: `owner`: some batch lies at slab 8 - 2, some at slab 1 and some at slab 8 // 2; the others favour low slabs. `order`: each batch number once. `root_inv`: symmetric. `gain_inv`: symmetric.
All inputs are finite; a program needn't handle non-finite values.
Results may differ from a plain program's by a relative error of at most 0.0001.
Values sent between devices are 32-bit elements; how exact they have to be, the bound alone decides.
No kernel may reach another device: no remote copies, remote signals or barrier semaphores. Data moves between devices by JAX's collectives and lax.ppermute only.
A program may use at most 64 MiB of HBM per device.

v0:
```python
import jax
import jax.numpy as jnp
from jax import lax
from jax.sharding import PartitionSpec as P

BATCHES = 16
REACH = 3


def shifted(value, axis, steps):
    count = lax.axis_size(axis)
    pairs = [(source, (source + steps) % count) for source in range(count)]
    return lax.ppermute(value, axis, pairs)


def product(left_side, right_side):
    return jnp.dot(
        left_side, right_side, precision=lax.Precision.HIGHEST, preferred_element_type=jnp.float32
    )


def prior_direct(masked):
    total = masked
    for step in range(1, REACH + 1):
        for sign_step in [step, -step]:
            total = total + shifted(masked, "gx", sign_step)
    return total


def local(anomalies, state_mean, obs_value, obs_cell, owner, order, root_inv, gain_inv):
    members, lon_dev, lat_dev, levels = anomalies.shape
    cell_count = lon_dev * lat_dev * levels
    quarter = obs_value.shape[1]
    obs_total = obs_cell.shape[1]
    slab_count = lax.axis_size("gx")
    band_count = lax.axis_size("gy")
    column = lax.axis_index("gx")
    band_index = lax.axis_index("gy")
    lon_total = slab_count * lon_dev
    lat_total = band_count * lat_dev
    taper_span = REACH * lon_dev + 1.0
    cell_ids = jnp.arange(cell_count, dtype=jnp.int32)
    cell_lon = column * lon_dev + cell_ids // (lat_dev * levels)
    cell_lat = band_index * lat_dev + cell_ids // levels % lat_dev
    obs_band = jnp.arange(obs_total, dtype=jnp.int32) // quarter

    def assimilate(batch_turn, carried):
        state_rows, mean_row = carried
        batch_id = order[batch_turn]
        root_slab = owner[batch_id]
        is_root = column == root_slab
        cells_of = obs_cell[batch_id]
        local_ids = lax.dynamic_slice_in_dim(cells_of, band_index * quarter, quarter)
        picked = jnp.take(state_rows, local_ids, axis=1)
        innovation = obs_value[batch_id] - jnp.take(mean_row, local_ids)
        root_rows = root_inv[batch_id]
        gain_rows = gain_inv[batch_id]
        joined = jnp.concatenate([picked, innovation[None, :]], axis=0)
        masked = jnp.where(is_root, joined, jnp.zeros_like(joined))
        joined = prior_direct(masked)
        picked, innovation = (joined[:members], joined[members])
        prior_all, innov_all = (
            lax.all_gather(picked, "gy", axis=1, tiled=True),
            lax.all_gather(innovation, "gy", axis=0, tiled=True),
        )
        weighted = product(prior_all, root_rows.T)
        gain_part = product(gain_rows, innov_all)
        weighted_all, gain_all = (
            lax.all_gather(weighted, "gy", axis=1, tiled=True),
            lax.all_gather(gain_part, "gy", axis=0, tiled=True),
        )
        obs_lon = root_slab * lon_dev + cells_of // (lat_dev * levels)
        obs_lat = obs_band * lat_dev + cells_of // levels % lat_dev
        slab_gap = jnp.abs(column - root_slab)
        in_reach = jnp.minimum(slab_gap, slab_count - slab_gap) <= REACH

        def near_update(operands):
            rows_now, mean_now = operands
            lon_gap = jnp.abs(obs_lon[:, None] - cell_lon[None, :])
            cycle_gap = jnp.minimum(lon_gap, lon_total - lon_gap)
            lat_gap = jnp.abs(obs_lat[:, None] - cell_lat[None, :])
            taper_rows = jnp.maximum(0.0, 1.0 - cycle_gap.astype(jnp.float32) / taper_span) * (
                1.0 - lat_gap.astype(jnp.float32) / lat_total
            )
            covariance = product(prior_all.T, rows_now) / (members - 1.0)
            gained = taper_rows * covariance
            stacked = jnp.concatenate([weighted_all, gain_all[None, :]], axis=0)
            increment = product(stacked, gained)
            return (rows_now - increment[:members], mean_now + increment[members])

        def keep_all(operands):
            return operands

        return lax.cond(in_reach, near_update, keep_all, (state_rows, mean_row))

    start_rows = anomalies.reshape(members, cell_count)
    start_mean = state_mean.reshape(cell_count)
    final_rows, final_mean = lax.fori_loop(0, BATCHES, assimilate, (start_rows, start_mean))
    return (
        final_rows.reshape(members, lon_dev, lat_dev, levels),
        final_mean.reshape(lon_dev, lat_dev, levels),
    )


def solution(mesh):
    return jax.shard_map(
        local,
        mesh=mesh,
        in_specs=(
            P(None, "gx", "gy", None),
            P("gx", "gy", None),
            P(None, "gy"),
            P(),
            P(),
            P(),
            P(None, "gy", None),
            P(None, "gy", None),
        ),
        out_specs=(P(None, "gx", "gy", None), P("gx", "gy", None)),
        check_vma=False,
    )
```

profile of v0, /device:TPU:13, one launch (start us, length us, event | category | flops | bytes accessed | tf_op | source)
XLA Modules:
  0.0 857.0 jit_solution(17424836850244703015)
XLA Ops:
  3.4 852.6 %while.19 = (s32[]{:T(128)}, f32[80,2048]{1,0:T(8,128)S(1)}, f32[2048]{0:T(1024)S(1)}, s32[16]{0:T(128)}, s32[16]{0:T(128)}, /*index=5*/s32[]{:T(128)}, s32[16,2...) while((s32[]{:T(128)}, f32[80,2048]{1,0:T(8,128)S(1)}, ...), condition=%wide.region_3.4_spmd.clone, body=%wide.region_0.3_spmd.clone.sunk | while | flops 1037555904 | bytes 10573724 | solution.py:98
  23.5 7.5 all-reduce.6
  32.2 5.7 all-reduce.7
  37.9 6.7 all_gather.48
  76.5 7.6 all-reduce.6
  85.3 5.6 all-reduce.7
  90.9 6.5 all_gather.48
  128.7 7.6 all-reduce.6
  137.5 5.6 all-reduce.7
  143.2 6.7 all_gather.48
  181.9 7.3 all-reduce.6
  190.4 5.6 all-reduce.7
  196.0 6.5 all_gather.48
  235.2 7.4 all-reduce.6
  243.9 5.6 all-reduce.7
  249.5 6.7 all_gather.48
  288.9 7.4 all-reduce.6
  297.6 5.6 all-reduce.7
  303.2 6.5 all_gather.48
  342.4 7.4 all-reduce.6
  351.0 5.6 all-reduce.7
  356.6 6.7 all_gather.48
  396.1 7.4 all-reduce.6
  404.7 5.6 all-reduce.7
  410.3 6.5 all_gather.48
  449.5 7.4 all-reduce.6
  458.2 5.6 all-reduce.7
  463.8 6.7 all_gather.48
  503.2 7.4 all-reduce.6
  511.9 5.6 all-reduce.7
  517.5 6.5 all_gather.48
  556.7 7.4 all-reduce.6
  565.3 5.6 all-reduce.7
  571.0 6.7 all_gather.48
  610.4 7.4 all-reduce.6
  619.0 5.6 all-reduce.7
  624.7 6.5 all_gather.48
  663.9 7.4 all-reduce.6
  672.5 5.6 all-reduce.7
  678.1 6.7 all_gather.48
  717.6 7.4 all-reduce.6
  731.8 6.5 all_gather.48
  771.0 7.4 all-reduce.6
  779.6 5.6 all-reduce.7
  785.3 6.7 all_gather.48
  823.6 7.2 all-reduce.6
  832.0 5.6 all-reduce.7
  837.7 6.5 all_gather.48
  (919 shorter events, 562.0 us)
Async XLA Ops:
  12.8 8.5 collective-permute-start.4
  13.0 8.3 collective-permute-start.3
  64.7 8.6 %collective-permute-start.4 = (f32[81,64]{0,1:T(8,128)S(1)}, f32[81,64]{0,1:T(8,128)S(1)}, u32[]{:S(2)}, u32[]{:S(2)}) collective-permute-start(f32[81,64]{0,1:T(8,128)S(1)} %maximum_select_fusion.2), channel_id=1, source_target_pairs={{0,28},{4,0},{8,4},{12,8},{16,12},{20,16},{24,20},{28,24},{1,29},{... | collective-permute-start | bytes 62216 | tf_op jit(solution)/shard_map/while/body/eval_jaxpr/ppermute | solution.py:13
  66.1 7.1 collective-permute-start.3
  117.4 8.8 %collective-permute-start.4 = (f32[81,64]{0,1:T(8,128)S(1)}, f32[81,64]{0,1:T(8,128)S(1)}, u32[]{:S(2)}, u32[]{:S(2)}) collective-permute-start(f32[81,64]{0,1:T(8,128)S(1)} %maximum_select_fusion.2), channel_id=1, source_target_pairs={{0,28},{4,0},{8,4},{12,8},{16,12},{20,16},{24,20},{28,24},{1,29},{... | collective-permute-start | bytes 62216 | tf_op jit(solution)/shard_map/while/body/eval_jaxpr/ppermute | solution.py:13
  118.8 7.3 collective-permute-start.3
  169.9 9.9 %collective-permute-start.4 = (f32[81,64]{0,1:T(8,128)S(1)}, f32[81,64]{0,1:T(8,128)S(1)}, u32[]{:S(2)}, u32[]{:S(2)}) collective-permute-start(f32[81,64]{0,1:T(8,128)S(1)} %maximum_select_fusion.2), channel_id=1, source_target_pairs={{0,28},{4,0},{8,4},{12,8},{16,12},{20,16},{24,20},{28,24},{1,29},{... | collective-permute-start | bytes 62216 | tf_op jit(solution)/shard_map/while/body/eval_jaxpr/ppermute | solution.py:13
  171.4 8.5 collective-permute-start.3
  172.4 7.4 collective-permute-start.2
  222.5 7.6 collective-permute-start.5
  222.5 10.8 %collective-permute-start.4 = (f32[81,64]{0,1:T(8,128)S(1)}, f32[81,64]{0,1:T(8,128)S(1)}, u32[]{:S(2)}, u32[]{:S(2)}) collective-permute-start(f32[81,64]{0,1:T(8,128)S(1)} %maximum_select_fusion.2), channel_id=1, source_target_pairs={{0,28},{4,0},{8,4},{12,8},{16,12},{20,16},{24,20},{28,24},{1,29},{... | collective-permute-start | bytes 62216 | tf_op jit(solution)/shard_map/while/body/eval_jaxpr/ppermute | solution.py:13
  224.0 9.3 %collective-permute-start.3 = (f32[81,64]{0,1:T(8,128)S(1)}, f32[81,64]{0,1:T(8,128)S(1)}, u32[]{:S(2)}, u32[]{:S(2)}) collective-permute-start(f32[81,64]{0,1:T(8,128)S(1)} %maximum_select_fusion.2), channel_id=1, source_target_pairs={{0,8},{4,12},{8,16},{12,20},{16,24},{20,28},{24,0},{28,4},{1,9},{5... | collective-permute-start | bytes 62216 | tf_op jit(solution)/shard_map/while/body/eval_jaxpr/ppermute | solution.py:13
  276.2 7.6 collective-permute-start.5
  276.2 10.8 %collective-permute-start.4 = (f32[81,64]{0,1:T(8,128)S(1)}, f32[81,64]{0,1:T(8,128)S(1)}, u32[]{:S(2)}, u32[]{:S(2)}) collective-permute-start(f32[81,64]{0,1:T(8,128)S(1)} %maximum_select_fusion.2), channel_id=1, source_target_pairs={{0,28},{4,0},{8,4},{12,8},{16,12},{20,16},{24,20},{28,24},{1,29},{... | collective-permute-start | bytes 62216 | tf_op jit(solution)/shard_map/while/body/eval_jaxpr/ppermute | solution.py:13
  277.7 9.3 %collective-permute-start.3 = (f32[81,64]{0,1:T(8,128)S(1)}, f32[81,64]{0,1:T(8,128)S(1)}, u32[]{:S(2)}, u32[]{:S(2)}) collective-permute-start(f32[81,64]{0,1:T(8,128)S(1)} %maximum_select_fusion.2), channel_id=1, source_target_pairs={{0,8},{4,12},{8,16},{12,20},{16,24},{20,28},{24,0},{28,4},{1,9},{5... | collective-permute-start | bytes 62216 | tf_op jit(solution)/shard_map/while/body/eval_jaxpr/ppermute | solution.py:13
  329.7 7.6 collective-permute-start.5
  329.7 10.8 %collective-permute-start.4 = (f32[81,64]{0,1:T(8,128)S(1)}, f32[81,64]{0,1:T(8,128)S(1)}, u32[]{:S(2)}, u32[]{:S(2)}) collective-permute-start(f32[81,64]{0,1:T(8,128)S(1)} %maximum_select_fusion.2), channel_id=1, source_target_pairs={{0,28},{4,0},{8,4},{12,8},{16,12},{20,16},{24,20},{28,24},{1,29},{... | collective-permute-start | bytes 62216 | tf_op jit(solution)/shard_map/while/body/eval_jaxpr/ppermute | solution.py:13
  331.1 9.3 %collective-permute-start.3 = (f32[81,64]{0,1:T(8,128)S(1)}, f32[81,64]{0,1:T(8,128)S(1)}, u32[]{:S(2)}, u32[]{:S(2)}) collective-permute-start(f32[81,64]{0,1:T(8,128)S(1)} %maximum_select_fusion.2), channel_id=1, source_target_pairs={{0,8},{4,12},{8,16},{12,20},{16,24},{20,28},{24,0},{28,4},{1,9},{5... | collective-permute-start | bytes 62216 | tf_op jit(solution)/shard_map/while/body/eval_jaxpr/ppermute | solution.py:13
  383.4 7.6 collective-permute-start.5
  383.4 10.8 %collective-permute-start.4 = (f32[81,64]{0,1:T(8,128)S(1)}, f32[81,64]{0,1:T(8,128)S(1)}, u32[]{:S(2)}, u32[]{:S(2)}) collective-permute-start(f32[81,64]{0,1:T(8,128)S(1)} %maximum_select_fusion.2), channel_id=1, source_target_pairs={{0,28},{4,0},{8,4},{12,8},{16,12},{20,16},{24,20},{28,24},{1,29},{... | collective-permute-start | bytes 62216 | tf_op jit(solution)/shard_map/while/body/eval_jaxpr/ppermute | solution.py:13
  384.8 9.3 %collective-permute-start.3 = (f32[81,64]{0,1:T(8,128)S(1)}, f32[81,64]{0,1:T(8,128)S(1)}, u32[]{:S(2)}, u32[]{:S(2)}) collective-permute-start(f32[81,64]{0,1:T(8,128)S(1)} %maximum_select_fusion.2), channel_id=1, source_target_pairs={{0,8},{4,12},{8,16},{12,20},{16,24},{20,28},{24,0},{28,4},{1,9},{5... | collective-permute-start | bytes 62216 | tf_op jit(solution)/shard_map/while/body/eval_jaxpr/ppermute | solution.py:13
  436.8 7.6 collective-permute-start.5
  436.8 10.8 %collective-permute-start.4 = (f32[81,64]{0,1:T(8,128)S(1)}, f32[81,64]{0,1:T(8,128)S(1)}, u32[]{:S(2)}, u32[]{:S(2)}) collective-permute-start(f32[81,64]{0,1:T(8,128)S(1)} %maximum_select_fusion.2), channel_id=1, source_target_pairs={{0,28},{4,0},{8,4},{12,8},{16,12},{20,16},{24,20},{28,24},{1,29},{... | collective-permute-start | bytes 62216 | tf_op jit(solution)/shard_map/while/body/eval_jaxpr/ppermute | solution.py:13
  438.3 9.3 %collective-permute-start.3 = (f32[81,64]{0,1:T(8,128)S(1)}, f32[81,64]{0,1:T(8,128)S(1)}, u32[]{:S(2)}, u32[]{:S(2)}) collective-permute-start(f32[81,64]{0,1:T(8,128)S(1)} %maximum_select_fusion.2), channel_id=1, source_target_pairs={{0,8},{4,12},{8,16},{12,20},{16,24},{20,28},{24,0},{28,4},{1,9},{5... | collective-permute-start | bytes 62216 | tf_op jit(solution)/shard_map/while/body/eval_jaxpr/ppermute | solution.py:13
  438.4 9.2 %collective-permute-start.2 = (f32[81,64]{0,1:T(8,128)S(1)}, f32[81,64]{0,1:T(8,128)S(1)}, u32[]{:S(2)}, u32[]{:S(2)}) collective-permute-start(f32[81,64]{0,1:T(8,128)S(1)} %maximum_select_fusion.2), channel_id=1, source_target_pairs={{0,24},{4,28},{8,0},{12,4},{16,8},{20,12},{24,16},{28,20},{1,25},{... | collective-permute-start | bytes 62216 | tf_op jit(solution)/shard_map/while/body/eval_jaxpr/ppermute | solution.py:13
  439.8 7.9 collective-permute-start.1
  490.5 7.6 collective-permute-start.5
  490.5 10.8 %collective-permute-start.4 = (f32[81,64]{0,1:T(8,128)S(1)}, f32[81,64]{0,1:T(8,128)S(1)}, u32[]{:S(2)}, u32[]{:S(2)}) collective-permute-start(f32[81,64]{0,1:T(8,128)S(1)} %maximum_select_fusion.2), channel_id=1, source_target_pairs={{0,28},{4,0},{8,4},{12,8},{16,12},{20,16},{24,20},{28,24},{1,29},{... | collective-permute-start | bytes 62216 | tf_op jit(solution)/shard_map/while/body/eval_jaxpr/ppermute | solution.py:13
  492.0 9.3 %collective-permute-start.3 = (f32[81,64]{0,1:T(8,128)S(1)}, f32[81,64]{0,1:T(8,128)S(1)}, u32[]{:S(2)}, u32[]{:S(2)}) collective-permute-start(f32[81,64]{0,1:T(8,128)S(1)} %maximum_select_fusion.2), channel_id=1, source_target_pairs={{0,8},{4,12},{8,16},{12,20},{16,24},{20,28},{24,0},{28,4},{1,9},{5... | collective-permute-start | bytes 62216 | tf_op jit(solution)/shard_map/while/body/eval_jaxpr/ppermute | solution.py:13
  544.0 7.6 collective-permute-start.5
  544.0 10.8 %collective-permute-start.4 = (f32[81,64]{0,1:T(8,128)S(1)}, f32[81,64]{0,1:T(8,128)S(1)}, u32[]{:S(2)}, u32[]{:S(2)}) collective-permute-start(f32[81,64]{0,1:T(8,128)S(1)} %maximum_select_fusion.2), channel_id=1, source_target_pairs={{0,28},{4,0},{8,4},{12,8},{16,12},{20,16},{24,20},{28,24},{1,29},{... | collective-permute-start | bytes 62216 | tf_op jit(solution)/shard_map/while/body/eval_jaxpr/ppermute | solution.py:13
  545.4 9.3 %collective-permute-start.3 = (f32[81,64]{0,1:T(8,128)S(1)}, f32[81,64]{0,1:T(8,128)S(1)}, u32[]{:S(2)}, u32[]{:S(2)}) collective-permute-start(f32[81,64]{0,1:T(8,128)S(1)} %maximum_select_fusion.2), channel_id=1, source_target_pairs={{0,8},{4,12},{8,16},{12,20},{16,24},{20,28},{24,0},{28,4},{1,9},{5... | collective-permute-start | bytes 62216 | tf_op jit(solution)/shard_map/while/body/eval_jaxpr/ppermute | solution.py:13
  597.7 7.6 collective-permute-start.5
  597.7 10.8 %collective-permute-start.4 = (f32[81,64]{0,1:T(8,128)S(1)}, f32[81,64]{0,1:T(8,128)S(1)}, u32[]{:S(2)}, u32[]{:S(2)}) collective-permute-start(f32[81,64]{0,1:T(8,128)S(1)} %maximum_select_fusion.2), channel_id=1, source_target_pairs={{0,28},{4,0},{8,4},{12,8},{16,12},{20,16},{24,20},{28,24},{1,29},{... | collective-permute-start | bytes 62216 | tf_op jit(solution)/shard_map/while/body/eval_jaxpr/ppermute | solution.py:13
  599.2 9.3 %collective-permute-start.3 = (f32[81,64]{0,1:T(8,128)S(1)}, f32[81,64]{0,1:T(8,128)S(1)}, u32[]{:S(2)}, u32[]{:S(2)}) collective-permute-start(f32[81,64]{0,1:T(8,128)S(1)} %maximum_select_fusion.2), channel_id=1, source_target_pairs={{0,8},{4,12},{8,16},{12,20},{16,24},{20,28},{24,0},{28,4},{1,9},{5... | collective-permute-start | bytes 62216 | tf_op jit(solution)/shard_map/while/body/eval_jaxpr/ppermute | solution.py:13
  651.1 7.6 collective-permute-start.5
  651.1 10.8 %collective-permute-start.4 = (f32[81,64]{0,1:T(8,128)S(1)}, f32[81,64]{0,1:T(8,128)S(1)}, u32[]{:S(2)}, u32[]{:S(2)}) collective-permute-start(f32[81,64]{0,1:T(8,128)S(1)} %maximum_select_fusion.2), channel_id=1, source_target_pairs={{0,28},{4,0},{8,4},{12,8},{16,12},{20,16},{24,20},{28,24},{1,29},{... | collective-permute-start | bytes 62216 | tf_op jit(solution)/shard_map/while/body/eval_jaxpr/ppermute | solution.py:13
  652.6 9.3 %collective-permute-start.3 = (f32[81,64]{0,1:T(8,128)S(1)}, f32[81,64]{0,1:T(8,128)S(1)}, u32[]{:S(2)}, u32[]{:S(2)}) collective-permute-start(f32[81,64]{0,1:T(8,128)S(1)} %maximum_select_fusion.2), channel_id=1, source_target_pairs={{0,8},{4,12},{8,16},{12,20},{16,24},{20,28},{24,0},{28,4},{1,9},{5... | collective-permute-start | bytes 62216 | tf_op jit(solution)/shard_map/while/body/eval_jaxpr/ppermute | solution.py:13
  704.8 7.6 collective-permute-start.5
  704.8 10.8 %collective-permute-start.4 = (f32[81,64]{0,1:T(8,128)S(1)}, f32[81,64]{0,1:T(8,128)S(1)}, u32[]{:S(2)}, u32[]{:S(2)}) collective-permute-start(f32[81,64]{0,1:T(8,128)S(1)} %maximum_select_fusion.2), channel_id=1, source_target_pairs={{0,28},{4,0},{8,4},{12,8},{16,12},{20,16},{24,20},{28,24},{1,29},{... | collective-permute-start | bytes 62216 | tf_op jit(solution)/shard_map/while/body/eval_jaxpr/ppermute | solution.py:13
  706.3 9.3 %collective-permute-start.3 = (f32[81,64]{0,1:T(8,128)S(1)}, f32[81,64]{0,1:T(8,128)S(1)}, u32[]{:S(2)}, u32[]{:S(2)}) collective-permute-start(f32[81,64]{0,1:T(8,128)S(1)} %maximum_select_fusion.2), channel_id=1, source_target_pairs={{0,8},{4,12},{8,16},{12,20},{16,24},{20,28},{24,0},{28,4},{1,9},{5... | collective-permute-start | bytes 62216 | tf_op jit(solution)/shard_map/while/body/eval_jaxpr/ppermute | solution.py:13
  706.5 9.2 %collective-permute-start.2 = (f32[81,64]{0,1:T(8,128)S(1)}, f32[81,64]{0,1:T(8,128)S(1)}, u32[]{:S(2)}, u32[]{:S(2)}) collective-permute-start(f32[81,64]{0,1:T(8,128)S(1)} %maximum_select_fusion.2), channel_id=1, source_target_pairs={{0,24},{4,28},{8,0},{12,4},{16,8},{20,12},{24,16},{28,20},{1,25},{... | collective-permute-start | bytes 62216 | tf_op jit(solution)/shard_map/while/body/eval_jaxpr/ppermute | solution.py:13
  707.8 7.9 collective-permute-start.1
  758.3 7.6 collective-permute-start.5
  758.3 10.8 %collective-permute-start.4 = (f32[81,64]{0,1:T(8,128)S(1)}, f32[81,64]{0,1:T(8,128)S(1)}, u32[]{:S(2)}, u32[]{:S(2)}) collective-permute-start(f32[81,64]{0,1:T(8,128)S(1)} %maximum_select_fusion.2), channel_id=1, source_target_pairs={{0,28},{4,0},{8,4},{12,8},{16,12},{20,16},{24,20},{28,24},{1,29},{... | collective-permute-start | bytes 62216 | tf_op jit(solution)/shard_map/while/body/eval_jaxpr/ppermute | solution.py:13
  759.8 9.3 %collective-permute-start.3 = (f32[81,64]{0,1:T(8,128)S(1)}, f32[81,64]{0,1:T(8,128)S(1)}, u32[]{:S(2)}, u32[]{:S(2)}) collective-permute-start(f32[81,64]{0,1:T(8,128)S(1)} %maximum_select_fusion.2), channel_id=1, source_target_pairs={{0,8},{4,12},{8,16},{12,20},{16,24},{20,28},{24,0},{28,4},{1,9},{5... | collective-permute-start | bytes 62216 | tf_op jit(solution)/shard_map/while/body/eval_jaxpr/ppermute | solution.py:13
  812.0 8.5 collective-permute-start.4
  813.5 7.1 collective-permute-start.3
  (65 other events, 551.3 us)
where the time goes:
time: 862 us; the launch traced here: 857 us
  blocking collectives  401 us (47%)
  starting transfers between devices  132 us (15%)
  local copies, waits for them, and re-layouts  113 us (13%)
  matrix products  103 us (12%)
  loops' own time  71.5 us (8%)
  waiting for transfers between devices  25.7 us (3%)
  other arithmetic  9.31 us (1%)
    ppermute x96, starting transfers between devices, shifted(): return lax.ppermute(value, axis, pairs)  132 us
    all_gather x16, blocking collectives, assimilate(): lax.all_gather(innovation, 'gy', axis=0, tiled=True)  119 us
    all_gather x16, blocking collectives, assimilate(): lax.all_gather(picked, 'gy', axis=1, tiled=True)  106 us
    dot_general x64, matrix products, product(): jnp.dot(left_side, right_side, precision=lax.Precision.HIGHEST, preferred...  103 us
    while x16, blocking collectives  90.2 us
    all_gather x16, blocking collectives, assimilate(): lax.all_gather(weighted, 'gy', axis=1, tiled=True)  86.7 us
    another operation x1, loops' own time, local(): lax.fori_loop(0, BATCHES, assimilate, (start_rows, start_mean))  60.9 us
    ppermute x96, waiting for transfers between devices, shifted(): return lax.ppermute(value, axis, pairs)  25.7 us
  transfers between devices with their start and end apart: 96, of which 16 were waited for; matrix products, arithmetic and copies ran while one was open for 1% of the time, Pallas kernels for 0%

commit v1 on v0

v1 whole, which is shorter than its diff:
```python
import functools
import jax
import jax.numpy as jnp
from jax import lax
from jax.experimental import pallas as pl
from jax.experimental.pallas import tpu as pltpu
from jax.sharding import PartitionSpec as P

REACH = 3
LANES = 128
CHUNK = 512
F32 = jnp.float32
BF16 = jnp.bfloat16


def swapped(value, axis, mask):
    count = lax.axis_size(axis)
    return lax.ppermute(value, axis, [(source, source ^ mask) for source in range(count)])


def split(value):
    high = value.astype(BF16).astype(F32)
    return high, value - high


def dot(left, right):
    return jnp.dot(left, right, preferred_element_type=F32)


def gather_kernel(
    dims, order, owner, place, cells, anom, mean, obs, own_out, keep_out, send_out, parts
):
    members, blocks, quarter, pairs = dims
    rows = own_out.shape[0]
    column, band = place[0], place[1]
    half = lax.rem(column, 2)
    for k in range(blocks):
        block = anom[pl.ds(k, members, stride=blocks), :]
        extra = jnp.concatenate(
            [-mean[k : k + 1, :], jnp.zeros((rows - members - 1, LANES), F32)], axis=0
        )
        block = jnp.concatenate([block, extra], axis=0)
        own_out[:, k * LANES : (k + 1) * LANES] = block
        high, rest = split(block)
        mid, low = split(rest)
        stack = jnp.concatenate([high, mid, low], axis=0)
        parts[:, k * LANES : (k + 1) * LANES] = stack.astype(BF16)
    lane = lax.broadcasted_iota(jnp.int32, (1, LANES), 1)
    first = lane < quarter
    total = cells.shape[1]
    shift = lax.rem(total - band * quarter, total)

    def ids_of(pair):
        even, odd = order[2 * pair], order[2 * pair + 1]
        row_even = pltpu.roll(cells[pl.ds(even, 1), :], shift, 1)[:, :LANES]
        row_odd = pltpu.roll(cells[pl.ds(odd, 1), :], lax.rem(shift + quarter, total), 1)
        row_odd = row_odd[:, :LANES]
        here_even = owner[even] == column
        here_odd = owner[odd] == column
        mine = jnp.where(first, here_even.astype(jnp.int32), here_odd.astype(jnp.int32))
        ids = jnp.where(mine > 0, jnp.where(first, row_even, row_odd), -1)
        seen = jnp.where(first, obs[pl.ds(even, 1), :], obs[pl.ds(odd, 1), :])
        seen = jnp.where(mine > 0, seen, 0.0)
        return ids, seen, jnp.logical_or(here_even, here_odd)

    for out, which in ((keep_out, half), (send_out, 1 - half)):
        for slot in range(0, pairs // 2, 2):
            pair = which * (pairs // 2) + slot
            ids_a, seen_a, any_a = ids_of(pair)
            ids_b, seen_b, any_b = ids_of(pair + 1)
            ids = jnp.concatenate([ids_a, ids_b], axis=1)
            seen = jnp.concatenate([seen_a, seen_b], axis=1)
            span = slice(slot * LANES, (slot + 2) * LANES)
            busy = jnp.logical_or(any_a, any_b)

            @pl.when(busy)
            def _(out=out, ids=ids, seen=seen, span=span):
                total_cells = parts.shape[1]
                cell = lax.broadcasted_iota(jnp.int32, (total_cells, 2 * LANES), 0)
                hot = jnp.where(cell == ids, 1.0, 0.0).astype(BF16)
                found = dot(parts[...], hot)
                value = found[:rows] + found[rows : 2 * rows] + found[2 * rows :]
                row = lax.broadcasted_iota(jnp.int32, value.shape, 0)
                out[:, span] = value + jnp.where(row == members, seen, 0.0)

            @pl.when(jnp.logical_not(busy))
            def _(out=out, span=span):
                out[:, span] = jnp.zeros((rows, 2 * LANES), F32)


def chain_kernel(
    dims,
    order,
    owner,
    place,
    cells,
    own,
    *refs,
):
    members, lon_dev, lat_dev, quarter, batches, slabs, bands = dims
    pieces = refs[:8]
    matrices = refs[8:16]
    anom_out, mean_out = refs[16:18]
    state, lon_at, lat_at, near, far, zcat, wcat, lat_of, bit_of, root, gain, sems = refs[18:]
    rows = state.shape[0]
    own_cells = own.shape[1]
    own_tiles = own_cells // LANES
    obs = 4 * quarter
    column, band = place[0], place[1]
    core = lax.rem(band, 2)
    chip = lax.div(band, 2)
    lat_total = float(bands * lat_dev)
    lon_total = float(slabs * lon_dev)
    reach_span = REACH * lon_dev + 1.0

    def loads(turn, slot):
        b = order[turn]
        near_cols = pl.ds(pl.multiple_of(chip * LANES, LANES), LANES)
        far_cols = pl.ds(pl.multiple_of((1 - chip) * LANES, LANES), LANES)
        mine = pl.multiple_of(core * quarter, quarter)
        theirs = pl.multiple_of((1 - core) * quarter, quarter)
        left, right = pl.ds(0, LANES), pl.ds(LANES, LANES)
        found = []
        for kind, buffer in ((0, root), (1, gain)):
            local, partner, across, relayed = matrices[4 * kind : 4 * kind + 4]
            plan = [
                (local.at[b, :, near_cols], mine, left),
                (local.at[b, :, far_cols], mine, right),
                (partner.at[b, :, near_cols], theirs, left),
                (partner.at[b, :, far_cols], theirs, right),
                (across.at[b], 2 * quarter + mine, right),
                (relayed.at[b], 2 * quarter + theirs, right),
            ]
            for source, row, cols in plan:
                sem = sems.at[slot, len(found)]
                target = buffer.at[slot, pl.ds(row, quarter), cols]
                found.append(pltpu.make_async_copy(source, target, sem))
        return found

    for copy in loads(0, 0):
        copy.start()

    state[:, :own_cells] = own[...]
    lane = lax.broadcasted_iota(jnp.int32, (1, LANES), 1)
    first = lane < quarter
    low_core = jnp.where(first, 1, 0) * jnp.where(core == 0, 1, 0) + jnp.where(
        first, 0, 1
    ) * jnp.where(core == 0, 0, 1)
    from_self = low_core > 0
    half_pairs = batches // 4
    half = lax.rem(column, 2)
    for which in range(2):
        pair_base = (half if which == 0 else 1 - half) * half_pairs
        for side in range(2):
            mine = pieces[2 * side + which]
            theirs = pieces[4 + 2 * side + which]
            for k in range(half_pairs):
                span = slice(k * LANES, (k + 1) * LANES)
                a, b = mine[:, span], theirs[:, span]
                a_roll, b_roll = pltpu.roll(a, quarter, 1), pltpu.roll(b, quarter, 1)
                a_first, b_first = (
                    jnp.where(core == 0, a, a_roll),
                    jnp.where(core == 0, b_roll, b),
                )
                a_last, b_last = (
                    jnp.where(core == 0, a_roll, a),
                    jnp.where(core == 0, b, b_roll),
                )
                turn = 2 * (pair_base + k)
                for step, (x, y) in enumerate(((a_first, b_first), (a_last, b_last))):
                    at = own_cells + (batches - 1 - turn - step) * obs + side * LANES
                    at = pl.multiple_of(at, LANES)
                    state[:, pl.ds(at, LANES)] = jnp.where(from_self, x, y)

    tile = lax.broadcasted_iota(jnp.int32, (own_tiles, LANES), 0)
    lon_at[:own_tiles, :] = (column * lon_dev + tile // lat_dev).astype(F32)
    lat_at[:own_tiles, :] = (band * lat_dev + tile % lat_dev).astype(F32) / lat_total

    @pl.loop(0, batches)
    def _(turn):
        b = order[turn]
        cells_row = cells[pl.ds(b, 1), :]
        for side in range(2):
            group = chip if side == 0 else 1 - chip
            cell = jnp.where(group == 0, cells_row[:, :LANES], cells_row[:, LANES:])
            level_band = lax.shift_right_logical(cell, (LANES - 1).bit_length())
            lat = group * 2 + jnp.where(first, 0, 1)
            lat = lat * lat_dev + lax.rem(level_band, lat_dev)
            lon = owner[b] * lon_dev + lax.div(level_band, lat_dev)
            row = own_tiles + (batches - 1 - turn) * 2 + side
            lon_at[pl.ds(row, 1), :] = lon.astype(F32)
            lat_at[pl.ds(row, 1), :] = lat.astype(F32) / lat_total

    @pl.loop(0, batches)
    def _(turn):
        slot = lax.rem(turn, 2)
        for copy in loads(turn, slot):
            copy.wait()

        @pl.when(turn + 1 < batches)
        def _():
            for copy in loads(turn + 1, 1 - slot):
                copy.start()

        slab = owner[order[turn]]

        def factor(lon):
            gap = jnp.abs(lon_at[...] - lon)
            gap = jnp.minimum(gap, lon_total - gap)
            return jnp.maximum(0.0, 1.0 - gap / reach_span)

        base = (slab * lon_dev).astype(F32)
        near[...] = factor(base)
        far[...] = factor(base + 1.0)
        for side in range(2):
            row = own_tiles + (batches - 1 - turn) * 2 + side
            lat_row = jnp.broadcast_to(lat_at[pl.ds(row, 1), :], (LANES, LANES))
            bit_row = jnp.broadcast_to(lon_at[pl.ds(row, 1), :] - base, (LANES, LANES))
            span = slice(side * LANES, (side + 1) * LANES)
            lat_of[span, :] = lat_row.T
            bit_of[span, :] = bit_row.T

        at = pl.multiple_of(own_cells + (batches - 1 - turn) * obs, obs)
        z = state[:, pl.ds(at, obs)]
        z_high, z_low = split(z[:members])
        pad = jnp.zeros((obs - 3 * members, obs), F32)
        zcat[...] = jnp.concatenate([z_high, z_high, z_low, pad], axis=0).T.astype(BF16)
        d_high, d_low = split(z[members:])

        def symmetric(buffer):
            top = buffer[slot, : 2 * quarter, :]
            corner = buffer[slot, 2 * quarter :, 2 * quarter :]
            bottom = jnp.concatenate([top[:, 2 * quarter :].T, corner], axis=1)
            high, low = split(jnp.concatenate([top, bottom], axis=0))
            return high.astype(BF16), low.astype(BF16)

        root_high, root_low = symmetric(root)
        gain_high, gain_low = symmetric(gain)

        def thrice(high, low, right_high, right_low):
            count = high.shape[0]
            both = dot(jnp.concatenate([high, low], axis=0).astype(BF16), right_high)
            return both[:count] + both[count:] + dot(high.astype(BF16), right_low)

        v = thrice(z_high, z_low, root_high, root_low)
        u = thrice(d_high, d_low, gain_high, gain_low)
        w = jnp.concatenate([v, u], axis=0) * (1.0 / (members - 1.0))
        w_high, w_low = split(w)
        wcat[...] = jnp.concatenate([w_high, w_low], axis=0).astype(BF16)

        width = own_cells + (batches - 1 - turn) * obs
        count = lax.div(width + CHUNK - 1, CHUNK)

        @pl.loop(0, count)
        def _(chunk):
            start = pl.multiple_of(chunk * CHUNK, CHUNK)
            now = state[:, pl.ds(start, CHUNK)]
            high, low = split(now[:members])
            zeros = jnp.zeros((obs - 3 * members, CHUNK), F32)
            right = jnp.concatenate([high, low, high, zeros], axis=0).astype(BF16)
            cov = dot(zcat[...], right)
            parts = []
            for k in range(CHUNK // LANES):
                row = chunk * (CHUNK // LANES) + k
                near_row = near[pl.ds(row, 1), :]
                far_row = far[pl.ds(row, 1), :]
                lat_row = lat_at[pl.ds(row, 1), :]
                lat_part = 1.0 - jnp.abs(lat_of[...] - lat_row)
                lon_part = jnp.where(bit_of[...] > 0.5, far_row, near_row)
                parts.append(cov[:, k * LANES : (k + 1) * LANES] * (lat_part * lon_part))
            gained = jnp.concatenate(parts, axis=1)
            g_high = gained.astype(BF16)
            g_low = (gained - g_high.astype(F32)).astype(BF16)
            both = dot(wcat[...], g_high)
            change = both[:rows] + both[rows:] + dot(wcat[:rows, :], g_low)
            state[:, pl.ds(start, CHUNK)] = now - change

    for k in range(own_tiles):
        span = slice(k * LANES, (k + 1) * LANES)
        anom_out[pl.ds(k, members, stride=own_tiles), :] = state[:members, span]
        mean_out[k : k + 1, :] = -state[members : members + 1, span]


def local(anomalies, state_mean, obs_value, obs_cell, owner, order, root_inv, gain_inv):
    members, lon_dev, lat_dev, levels = anomalies.shape
    batches, quarter = obs_value.shape
    obs = obs_cell.shape[1]
    blocks = lon_dev * lat_dev
    own_cells = blocks * levels
    slabs = lax.axis_size("gx")
    bands = lax.axis_size("gy")
    column = lax.axis_index("gx")
    band = lax.axis_index("gy")
    rows = -(-(members + 1) // 8) * 8
    tiles = (own_cells + batches * obs) // LANES
    place = jnp.stack([column, band]).astype(jnp.int32)

    start = lax.div(band, 2) * 2 * quarter
    cut = functools.partial(
        lax.dynamic_slice_in_dim, start_index=start, slice_size=2 * quarter, axis=2
    )
    sent = [cut(root_inv), cut(gain_inv)]
    matrices = [
        [root_inv, swapped(root_inv, "gy", 1), swapped(sent[0], "gy", 2)],
        [gain_inv, swapped(gain_inv, "gy", 1), swapped(sent[1], "gy", 2)],
    ]
    for group in matrices:
        group.append(swapped(group[2], "gy", 1))

    smem = pl.BlockSpec(memory_space=pltpu.SMEM)
    vmem = pl.BlockSpec(memory_space=pltpu.VMEM)
    hbm = pl.BlockSpec(memory_space=pl.ANY)
    pairs = batches // 2
    piece = jax.ShapeDtypeStruct((rows, pairs // 2 * LANES), F32)
    own, keep, send = pl.pallas_call(
        functools.partial(gather_kernel, (members, blocks, quarter, pairs)),
        out_shape=(jax.ShapeDtypeStruct((rows, own_cells), F32), piece, piece),
        in_specs=[smem, smem, smem, vmem, vmem, vmem, vmem],
        out_specs=(vmem, vmem, vmem),
        scratch_shapes=[pltpu.VMEM((3 * rows, own_cells), BF16)],
        name="gather_observations",
    )(
        order,
        owner,
        place,
        obs_cell,
        anomalies.reshape(members * blocks, levels),
        state_mean.reshape(blocks, levels),
        jnp.concatenate([obs_value, obs_value], axis=1),
    )

    mine = keep + swapped(send, "gx", 1)
    mask = 2
    while mask < slabs:
        mine = mine + swapped(mine, "gx", mask)
        mask *= 2
    other = swapped(mine, "gx", 1)
    chip = [mine, other, swapped(mine, "gy", 2), swapped(other, "gy", 2)]
    pieces = chip + [swapped(part, "gy", 1) for part in chip]

    dims = (members, lon_dev, lat_dev, quarter, batches, slabs, bands)
    post, post_mean = pl.pallas_call(
        functools.partial(chain_kernel, dims),
        out_shape=(
            jax.ShapeDtypeStruct((members * blocks, levels), F32),
            jax.ShapeDtypeStruct((blocks, levels), F32),
        ),
        in_specs=[smem, smem, smem] + [vmem] * 10 + [hbm] * 8,
        out_specs=(vmem, vmem),
        scratch_shapes=[
            pltpu.VMEM((rows, own_cells + batches * obs), F32),
            pltpu.VMEM((tiles, LANES), F32),
            pltpu.VMEM((tiles, LANES), F32),
            pltpu.VMEM((tiles, LANES), F32),
            pltpu.VMEM((tiles, LANES), F32),
            pltpu.VMEM((obs, obs), BF16),
            pltpu.VMEM((2 * rows, obs), BF16),
            pltpu.VMEM((obs, LANES), F32),
            pltpu.VMEM((obs, LANES), F32),
            pltpu.VMEM((2, obs, obs), F32),
            pltpu.VMEM((2, obs, obs), F32),
            pltpu.SemaphoreType.DMA((2, 12)),
        ],
        name="observation_recursion",
    )(order, owner, place, obs_cell, own, *pieces, *matrices[0], *matrices[1])
    return (
        post.reshape(members, lon_dev, lat_dev, levels),
        post_mean.reshape(lon_dev, lat_dev, levels),
    )


def solution(mesh):
    return jax.shard_map(
        local,
        mesh=mesh,
        in_specs=(
            P(None, "gx", "gy", None),
            P("gx", "gy", None),
            P(None, "gy"),
            P(),
            P(),
            P(),
            P(None, "gy", None),
            P(None, "gy", None),
        ),
        out_specs=(P(None, "gx", "gy", None), P("gx", "gy", None)),
        check_vma=False,
    )
```

time: 862 us -> 118 us (0.14)
  blocking collectives: 401 us -> 0 us
  starting transfers between devices: 132 us -> 17.7 us
  local copies, waits for them, and re-layouts: 113 us -> 3.85 us
  matrix products: 103 us -> 0 us
  Pallas kernels: 0 us -> 71.5 us
  loops' own time: 71.5 us -> 0 us
    all_gather x48 -> x0, blocking collectives: 311 us -> none  [the longest x16 119 us: assimilate(): lax.all_gather(innovation, 'gy', axis=0, tiled=True)]
    ppermute x96 -> x16, starting transfers between devices: 132 us -> 17.7 us  [swapped(): lax.ppermute(value, axis, [(source, source ^ mask) for source in range(co...]
    dot_general x64 -> x0, matrix products: 103 us -> none  [product(): jnp.dot(left_side, right_side, precision=lax.Precision.HIGHEST, preferred...]
    while x16 -> x0, blocking collectives: 90.2 us -> none
    another operation x17 -> x0, loops' own time: 71.5 us -> none  [the longest x1 60.9 us: local(): lax.fori_loop(0, BATCHES, assimilate, (start_rows, start_mean))]
    pallas_call x0 -> x2, Pallas kernels: none -> 71.5 us  [the longest x1 67.8 us: local(): pl.pallas_call(functools.partial(chain_kernel, dims), out_shape=(jax.Shap...]
    dynamic_slice x96 -> x2, local copies, waits for them, and re-layouts: 59.2 us -> 1.15 us  [local(): sent = [cut(root_inv), cut(gain_inv)]]
    gather x48 -> x0, local copies, waits for them, and re-layouts: 23.6 us -> none  [the longest x32 14 us: assimilate(): innovation = obs_value[batch_id] - jnp.take(mean_row, local_ids)]
  transfers between devices with their start and end apart: 96 -> 16, of which waited for: 16 -> 7; matrix products, arithmetic and copies ran while one was open for 1% -> 1% of each run, Pallas kernels for 0% -> 0%
where the time goes in v1:
time: 118 us; the launch traced here: 116 us
  Pallas kernels  71.5 us (61%)
  waiting for transfers between devices  20.4 us (17%)
  starting transfers between devices  17.7 us (15%)
  local copies, waits for them, and re-layouts  3.85 us (3%)
  other arithmetic  1.4 us (1%)
    pallas_call x1, Pallas kernels, local(): pl.pallas_call(functools.partial(chain_kernel, dims), out_shape=(jax.Shap...  67.8 us
    ppermute x16, waiting for transfers between devices, swapped(): lax.ppermute(value, axis, [(source, source ^ mask) for source in range(co...  20.4 us
    ppermute x16, starting transfers between devices, swapped(): lax.ppermute(value, axis, [(source, source ^ mask) for source in range(co...  17.7 us
    pallas_call x1, Pallas kernels, local(): pl.pallas_call(functools.partial(gather_kernel, (members, blocks, quarter...  3.73 us
    unnamed x32, local copies, waits for them, and re-layouts  2.69 us
  transfers between devices with their start and end apart: 16, of which 7 were waited for; matrix products, arithmetic and copies ran while one was open for 1% of the time, Pallas kernels for 0%

profile of v1, /device:TPU:13, one launch (start us, length us, event | category | flops | bytes accessed | tf_op | source)
XLA Modules:
  0.0 115.6 jit_solution(953612914596200060)
XLA Ops:
  0.6 0.0 copy-start.15
  0.6 0.7 copy-done.15
  1.3 0.7 pad_maximum_fusion.obs
  2.0 0.6 pad_add_fusion.place
  2.7 3.7 %gather_observations.1 = (f32[88,2048]{1,0:T(8,128)}, f32[88,512]{1,0:T(8,128)}, f32[88,512]{1,0:T(8,128)}) custom-call(s32[16]{0:T(128)} %order.3, s32[16]{0:T(128)} %owner.3, s32[2]{0:T(128)} %pad_add_fusion.place, s32[16,256]{1,0:T(8,128)} %cells.3, f32[1280,128]{1,0:T(8,128)} %bitcast.6, f32[16,128]{1,0:T(8,128)} %bitcast.7, f32[16,128]{1,0:T(8,128)} %pad_maximum_fusion.obs), custom_call_target="tpu_custom_call" | custom-call | tf_op jit(solution)/shard_map/gather_observations/pallas_call | solution.py:315
  6.4 0.2 collective-permute-start
  6.6 1.1 constant_dynamic-slice_fusion
  7.7 1.3 %collective-permute-start.14 = (f32[16,64,128]{2,1,0:T(8,128)S(1)}, f32[16,64,128]{2,1,0:T(8,128)S(1)}, u32[]{:S(2)}, u32[]{:S(2)}) collective-permute-start(f32[16,64,128]{2,1,0:T(8,128)S(1)} %constant_dynamic-slice_fusion), channel_id=1, source_target_pairs={{0,2},{1,3},{2,0},{3,1},{4,6},{5,7},{6,4},{7,5},{8,10},{9,11},{10,... | collective-permute-start | bytes 1572872 | tf_op jit(solution)/shard_map/ppermute | solution.py:18
  9.0 3.0 %collective-permute-done = f32[88,512]{1,0:T(8,128)S(1)} collective-permute-done((f32[88,512]{1,0:T(8,128)}, f32[88,512]{1,0:T(8,128)S(1)}, u32[]{:S(2)}, u32[]{:S(2)}) %collective-permute-start) | collective-permute-done | bytes 180256 | tf_op jit(solution)/shard_map/ppermute | solution.py:18
  12.0 0.0 copy-done.9
  12.1 0.7 collective-permute-start.1
  12.8 0.0 copy-done
  12.8 1.3 %collective-permute-start.11 = (f32[16,64,128]{2,1,0:T(8,128)S(1)}, f32[16,64,128]{2,1,0:T(8,128)S(1)}, u32[]{:S(2)}, u32[]{:S(2)}) collective-permute-start(f32[16,64,128]{2,1,0:T(8,128)S(1)} %constant_dynamic-slice_fusion.1), channel_id=1, source_target_pairs={{0,2},{1,3},{2,0},{3,1},{4,6},{5,7},{6,4},{7,5},{8,10},{9,11},{10,... | collective-permute-start | bytes 1572872 | tf_op jit(solution)/shard_map/ppermute | solution.py:18
  14.1 2.7 %collective-permute-done.1 = f32[88,512]{1,0:T(8,128)S(1)} collective-permute-done((f32[88,512]{1,0:T(8,128)S(1)}, f32[88,512]{1,0:T(8,128)S(1)}, u32[]{:S(2)}, u32[]{:S(2)}) %collective-permute-start.1) | collective-permute-done | bytes 180256 | tf_op jit(solution)/shard_map/ppermute | solution.py:18
  16.8 1.5 %collective-permute-start.2 = (f32[88,512]{1,0:T(8,128)S(1)}, f32[88,512]{1,0:T(8,128)S(1)}, u32[]{:S(2)}, u32[]{:S(2)}) collective-permute-start(f32[88,512]{1,0:T(8,128)S(1)} %add.14), channel_id=1, source_target_pairs={{0,16},{4,20},{8,24},{12,28},{16,0},{20,4},{24,8},{28,12},{1,17},{... | collective-permute-start | bytes 540680 | tf_op jit(solution)/shard_map/ppermute | solution.py:18
  18.2 2.7 %collective-permute-start.10 = (f32[16,64,256]{2,1,0:T(8,128)S(1)}, f32[16,64,256]{2,1,0:T(8,128)S(1)}, u32[]{:S(2)}, u32[]{:S(2)}) collective-permute-start(f32[16,64,256]{2,1,0:T(8,128)S(1)} %copy-done), channel_id=1, source_target_pairs={{0,1},{1,0},{2,3},{3,2},{4,5},{5,4},{6,7},{7,6},{8,9},{9,8},{10,11... | collective-permute-start | bytes 3145736 | tf_op jit(solution)/shard_map/ppermute | solution.py:18
  20.9 0.0 copy-done.1
  20.9 0.0 collective-permute-start.13
  20.9 4.6 %collective-permute-done.2 = f32[88,512]{1,0:T(8,128)S(1)} collective-permute-done((f32[88,512]{1,0:T(8,128)S(1)}, f32[88,512]{1,0:T(8,128)S(1)}, u32[]{:S(2)}, u32[]{:S(2)}) %collective-permute-start.2) | collective-permute-done | bytes 180256 | tf_op jit(solution)/shard_map/ppermute | solution.py:18
  25.6 0.0 copy-start.4
  25.6 1.3 %collective-permute-start.4 = (f32[88,512]{1,0:T(8,128)S(1)}, f32[88,512]{1,0:T(8,128)S(1)}, u32[]{:S(2)}, u32[]{:S(2)}) collective-permute-start(f32[88,512]{1,0:T(8,128)S(1)} %add.15.refs_0_), channel_id=1, source_target_pairs={{0,2},{1,3},{2,0},{3,1},{4,6},{5,7},{6,4},{7,5},{8,10},{9,11},{10,... | collective-permute-start | bytes 540680 | tf_op jit(solution)/shard_map/ppermute | solution.py:18
  26.9 0.0 collective-permute-done.14.refs_14_
  26.9 0.7 collective-permute-start.3
  27.6 4.0 %collective-permute-done.11.refs_10_ = f32[16,64,128]{2,1,0:T(8,128)S(1)} collective-permute-done((f32[16,64,128]{2,1,0:T(8,128)S(1)}, f32[16,64,128]{2,1,0:T(8,128)S(1)}, u32[]{:S(2)}, u32[]{:S(2)}) %collective-permute-start.11) | collective-permute-done | bytes 524320 | tf_op jit(solution)/shard_map/ppermute | solution.py:18
  31.6 3.2 %collective-permute-start.6 = (f32[88,512]{1,0:T(8,128)S(1)}, f32[88,512]{1,0:T(8,128)}, u32[]{:S(2)}, u32[]{:S(2)}) collective-permute-start(f32[88,512]{1,0:T(8,128)S(1)} %add.15.refs_0_), channel_id=1, source_target_pairs={{0,1},{1,0},{2,3},{3,2},{4,5},{5,4},{6,7},{7,6},{8,9},{9,8},{10,11... | collective-permute-start | bytes 540680 | tf_op jit(solution)/shard_map/ppermute | solution.py:18
  34.8 0.6 collective-permute-done.4.refs_2_
  35.4 1.8 %collective-permute-start.8 = (f32[88,512]{1,0:T(8,128)S(1)}, f32[88,512]{1,0:T(8,128)}, u32[]{:S(2)}, u32[]{:S(2)}) collective-permute-start(f32[88,512]{1,0:T(8,128)S(1)} %collective-permute-done.4.refs_2_), channel_id=1, source_target_pairs={{0,1},{1,0},{2,3},{3,2},{4,5},{5,4},{6,7},{7,6},{8,9},{9,8},{10,11... | collective-permute-start | bytes 540680 | tf_op jit(solution)/shard_map/ppermute | solution.py:18
  37.2 0.0 collective-permute-done.3.refs_1_
  37.2 0.1 collective-permute-start.7
  37.3 0.0 collective-permute-done.6.refs_4_
  37.3 0.4 collective-permute-start.15
  37.8 0.7 collective-permute-done.8.refs_6_
  38.4 0.4 collective-permute-start.12
  38.8 0.0 collective-permute-done.7.refs_5_
  38.8 1.2 %collective-permute-start.5 = (f32[88,512]{1,0:T(8,128)S(1)}, f32[88,512]{1,0:T(8,128)S(1)}, u32[]{:S(2)}, u32[]{:S(2)}) collective-permute-start(f32[88,512]{1,0:T(8,128)S(1)} %collective-permute-done.3.refs_1_), channel_id=1, source_target_pairs={{0,2},{1,3},{2,0},{3,1},{4,6},{5,7},{6,4},{7,5},{8,10},{9,11},{10,... | collective-permute-start | bytes 540680 | tf_op jit(solution)/shard_map/ppermute | solution.py:18
  40.0 4.8 %collective-permute-done.5.refs_3_ = f32[88,512]{1,0:T(8,128)S(1)} collective-permute-done((f32[88,512]{1,0:T(8,128)S(1)}, f32[88,512]{1,0:T(8,128)S(1)}, u32[]{:S(2)}, u32[]{:S(2)}) %collective-permute-start.5) | collective-permute-done | bytes 180256 | tf_op jit(solution)/shard_map/ppermute | solution.py:18
  44.8 1.0 collective-permute-start.9
  45.8 0.0 collective-permute-done.15.refs_15_
  45.8 0.0 collective-permute-done.12.refs_11_
  45.8 0.0 copy-start.8
  45.8 0.0 collective-permute-done.10.refs_9_
  45.8 0.0 collective-permute-done.13.refs_13_
  45.8 1.0 copy-done.3
  46.9 0.0 collective-permute-done.9.refs_7_
  46.9 0.0 copy-done.7
  46.9 0.2 copy-done.8
  47.2 0.7 copy-done.14
  47.8 67.8 %observation_recursion.1 = (f32[1280,128]{1,0:T(8,128)}, f32[16,128]{1,0:T(8,128)}) custom-call(s32[16]{0:T(128)} %order.3, s32[16]{0:T(128)} %owner.3, s32[2]{0:T(128)} %pad_add_fusion.place, s32[16,256]{1,0:T(8,128)} %cells.3, f32[88,2048]{1,0:T(8,128)} %get-tuple-element.7.own, f32[88,512]{1,0:T(8,128)} %copy-done.4, f32[88,512]{1,0:T(8,128)} %copy-done.11, ...), custom_call_target="tpu_custom_call" | custom-call | tf_op jit(solution)/shard_map/observation_recursion/pallas_call | solution.py:342
  (25 shorter events, 0.1 us)
Async XLA Ops:
  0.6 0.7 copy-start.15
  2.6 10.1 %copy-start = (f32[16,64,256]{2,1,0:T(8,128)S(1)}, f32[16,64,256]{2,1,0:T(8,128)}, u32[]{:S(2)}) copy-start(f32[16,64,256]{2,1,0:T(8,128)} %refs_8_.1) | copy-start | bytes 3145732
  6.4 5.6 %collective-permute-start = (f32[88,512]{1,0:T(8,128)}, f32[88,512]{1,0:T(8,128)S(1)}, u32[]{:S(2)}, u32[]{:S(2)}) collective-permute-start(f32[88,512]{1,0:T(8,128)} %get-tuple-element.9), channel_id=1, source_target_pairs={{0,4},{4,0},{8,12},{12,8},{16,20},{20,16},{24,28},{28,24},{1,5},{5... | collective-permute-start | bytes 540680 | tf_op jit(solution)/shard_map/ppermute | solution.py:18
  6.6 5.4 %copy-start.9 = (f32[88,512]{1,0:T(8,128)S(1)}, f32[88,512]{1,0:T(8,128)}, u32[]{:S(2)}) copy-start(f32[88,512]{1,0:T(8,128)} %get-tuple-element.8) | copy-start | bytes 540676
  7.7 19.1 %collective-permute-start.14 = (f32[16,64,128]{2,1,0:T(8,128)S(1)}, f32[16,64,128]{2,1,0:T(8,128)S(1)}, u32[]{:S(2)}, u32[]{:S(2)}) collective-permute-start(f32[16,64,128]{2,1,0:T(8,128)S(1)} %constant_dynamic-slice_fusion), channel_id=1, source_target_pairs={{0,2},{1,3},{2,0},{3,1},{4,6},{5,7},{6,4},{7,5},{8,10},{9,11},{10,... | collective-permute-start | bytes 1572872 | tf_op jit(solution)/shard_map/ppermute | solution.py:18
  12.0 8.9 %copy-start.1 = (f32[16,64,256]{2,1,0:T(8,128)S(1)}, f32[16,64,256]{2,1,0:T(8,128)}, u32[]{:S(2)}) copy-start(f32[16,64,256]{2,1,0:T(8,128)} %refs_12_.1) | copy-start | bytes 3145732
  12.1 4.7 %collective-permute-start.1 = (f32[88,512]{1,0:T(8,128)S(1)}, f32[88,512]{1,0:T(8,128)S(1)}, u32[]{:S(2)}, u32[]{:S(2)}) collective-permute-start(f32[88,512]{1,0:T(8,128)S(1)} %add.13), channel_id=1, source_target_pairs={{0,8},{4,12},{8,0},{12,4},{16,24},{20,28},{24,16},{28,20},{1,9},{5... | collective-permute-start | bytes 540680 | tf_op jit(solution)/shard_map/ppermute | solution.py:18
  12.8 18.8 %collective-permute-start.11 = (f32[16,64,128]{2,1,0:T(8,128)S(1)}, f32[16,64,128]{2,1,0:T(8,128)S(1)}, u32[]{:S(2)}, u32[]{:S(2)}) collective-permute-start(f32[16,64,128]{2,1,0:T(8,128)S(1)} %constant_dynamic-slice_fusion.1), channel_id=1, source_target_pairs={{0,2},{1,3},{2,0},{3,1},{4,6},{5,7},{6,4},{7,5},{8,10},{9,11},{10,... | collective-permute-start | bytes 1572872 | tf_op jit(solution)/shard_map/ppermute | solution.py:18
  16.8 8.8 %collective-permute-start.2 = (f32[88,512]{1,0:T(8,128)S(1)}, f32[88,512]{1,0:T(8,128)S(1)}, u32[]{:S(2)}, u32[]{:S(2)}) collective-permute-start(f32[88,512]{1,0:T(8,128)S(1)} %add.14), channel_id=1, source_target_pairs={{0,16},{4,20},{8,24},{12,28},{16,0},{20,4},{24,8},{28,12},{1,17},{... | collective-permute-start | bytes 540680 | tf_op jit(solution)/shard_map/ppermute | solution.py:18
  18.2 27.5 %collective-permute-start.10 = (f32[16,64,256]{2,1,0:T(8,128)S(1)}, f32[16,64,256]{2,1,0:T(8,128)S(1)}, u32[]{:S(2)}, u32[]{:S(2)}) collective-permute-start(f32[16,64,256]{2,1,0:T(8,128)S(1)} %copy-done), channel_id=1, source_target_pairs={{0,1},{1,0},{2,3},{3,2},{4,5},{5,4},{6,7},{7,6},{8,9},{9,8},{10,11... | collective-permute-start | bytes 3145736 | tf_op jit(solution)/shard_map/ppermute | solution.py:18
  20.9 24.9 %collective-permute-start.13 = (f32[16,64,256]{2,1,0:T(8,128)S(1)}, f32[16,64,256]{2,1,0:T(8,128)S(1)}, u32[]{:S(2)}, u32[]{:S(2)}) collective-permute-start(f32[16,64,256]{2,1,0:T(8,128)S(1)} %copy-done.1), channel_id=1, source_target_pairs={{0,1},{1,0},{2,3},{3,2},{4,5},{5,4},{6,7},{7,6},{8,9},{9,8},{10,11... | collective-permute-start | bytes 3145736 | tf_op jit(solution)/shard_map/ppermute | solution.py:18
  25.6 22.2 %copy-start.4 = (f32[88,512]{1,0:T(8,128)}, f32[88,512]{1,0:T(8,128)S(1)}, u32[]{:S(2)}) copy-start(f32[88,512]{1,0:T(8,128)S(1)} %add.15.refs_0_) | copy-start | bytes 540676
  25.6 9.8 %collective-permute-start.4 = (f32[88,512]{1,0:T(8,128)S(1)}, f32[88,512]{1,0:T(8,128)S(1)}, u32[]{:S(2)}, u32[]{:S(2)}) collective-permute-start(f32[88,512]{1,0:T(8,128)S(1)} %add.15.refs_0_), channel_id=1, source_target_pairs={{0,2},{1,3},{2,0},{3,1},{4,6},{5,7},{6,4},{7,5},{8,10},{9,11},{10,... | collective-permute-start | bytes 540680 | tf_op jit(solution)/shard_map/ppermute | solution.py:18
  26.9 20.0 %copy-start.5 = (f32[16,64,128]{2,1,0:T(8,128)}, f32[16,64,128]{2,1,0:T(8,128)S(1)}, u32[]{:S(2)}) copy-start(f32[16,64,128]{2,1,0:T(8,128)S(1)} %collective-permute-done.14.refs_14_) | copy-start | bytes 1572868
  26.9 10.4 %collective-permute-start.3 = (f32[88,512]{1,0:T(8,128)S(1)}, f32[88,512]{1,0:T(8,128)S(1)}, u32[]{:S(2)}, u32[]{:S(2)}) collective-permute-start(f32[88,512]{1,0:T(8,128)S(1)} %add.15.refs_0_), channel_id=1, source_target_pairs={{0,4},{4,0},{8,12},{12,8},{16,20},{20,16},{24,28},{28,24},{1,5},{5... | collective-permute-start | bytes 540680 | tf_op jit(solution)/shard_map/ppermute | solution.py:18
  31.6 15.3 %copy-start.6 = (f32[16,64,128]{2,1,0:T(8,128)}, f32[16,64,128]{2,1,0:T(8,128)S(1)}, u32[]{:S(2)}) copy-start(f32[16,64,128]{2,1,0:T(8,128)S(1)} %collective-permute-done.11.refs_10_) | copy-start | bytes 1572868
  31.6 5.8 %collective-permute-start.6 = (f32[88,512]{1,0:T(8,128)S(1)}, f32[88,512]{1,0:T(8,128)}, u32[]{:S(2)}, u32[]{:S(2)}) collective-permute-start(f32[88,512]{1,0:T(8,128)S(1)} %add.15.refs_0_), channel_id=1, source_target_pairs={{0,1},{1,0},{2,3},{3,2},{4,5},{5,4},{6,7},{7,6},{8,9},{9,8},{10,11... | collective-permute-start | bytes 540680 | tf_op jit(solution)/shard_map/ppermute | solution.py:18
  35.4 12.4 %copy-start.10 = (f32[88,512]{1,0:T(8,128)}, f32[88,512]{1,0:T(8,128)S(1)}, u32[]{:S(2)}) copy-start(f32[88,512]{1,0:T(8,128)S(1)} %collective-permute-done.4.refs_2_) | copy-start | bytes 540676
  35.4 3.0 %collective-permute-start.8 = (f32[88,512]{1,0:T(8,128)S(1)}, f32[88,512]{1,0:T(8,128)}, u32[]{:S(2)}, u32[]{:S(2)}) collective-permute-start(f32[88,512]{1,0:T(8,128)S(1)} %collective-permute-done.4.refs_2_), channel_id=1, source_target_pairs={{0,1},{1,0},{2,3},{3,2},{4,5},{5,4},{6,7},{7,6},{8,9},{9,8},{10,11... | collective-permute-start | bytes 540680 | tf_op jit(solution)/shard_map/ppermute | solution.py:18
  37.2 9.6 %copy-start.11 = (f32[88,512]{1,0:T(8,128)}, f32[88,512]{1,0:T(8,128)S(1)}, u32[]{:S(2)}) copy-start(f32[88,512]{1,0:T(8,128)S(1)} %collective-permute-done.3.refs_1_) | copy-start | bytes 540676
  37.2 1.5 %collective-permute-start.7 = (f32[88,512]{1,0:T(8,128)S(1)}, f32[88,512]{1,0:T(8,128)S(1)}, u32[]{:S(2)}, u32[]{:S(2)}) collective-permute-start(f32[88,512]{1,0:T(8,128)S(1)} %collective-permute-done.3.refs_1_), channel_id=1, source_target_pairs={{0,1},{1,0},{2,3},{3,2},{4,5},{5,4},{6,7},{7,6},{8,9},{9,8},{10,11... | collective-permute-start | bytes 540680 | tf_op jit(solution)/shard_map/ppermute | solution.py:18
  37.3 8.4 %collective-permute-start.15 = (f32[16,64,128]{2,1,0:T(8,128)S(1)}, f32[16,64,128]{2,1,0:T(8,128)S(1)}, u32[]{:S(2)}, u32[]{:S(2)}) collective-permute-start(f32[16,64,128]{2,1,0:T(8,128)S(1)} %collective-permute-done.14.refs_14_), channel_id=1, source_target_pairs={{0,1},{1,0},{2,3},{3,2},{4,5},{5,4},{6,7},{7,6},{8,9},{9,8},{10,11... | collective-permute-start | bytes 1572872 | tf_op jit(solution)/shard_map/ppermute | solution.py:18
  38.4 7.4 %collective-permute-start.12 = (f32[16,64,128]{2,1,0:T(8,128)S(1)}, f32[16,64,128]{2,1,0:T(8,128)S(1)}, u32[]{:S(2)}, u32[]{:S(2)}) collective-permute-start(f32[16,64,128]{2,1,0:T(8,128)S(1)} %collective-permute-done.11.refs_10_), channel_id=1, source_target_pairs={{0,1},{1,0},{2,3},{3,2},{4,5},{5,4},{6,7},{7,6},{8,9},{9,8},{10,11... | collective-permute-start | bytes 1572872 | tf_op jit(solution)/shard_map/ppermute | solution.py:18
  38.8 8.1 %copy-start.12 = (f32[88,512]{1,0:T(8,128)}, f32[88,512]{1,0:T(8,128)S(1)}, u32[]{:S(2)}) copy-start(f32[88,512]{1,0:T(8,128)S(1)} %collective-permute-done.7.refs_5_) | copy-start | bytes 540676
  38.8 6.0 %collective-permute-start.5 = (f32[88,512]{1,0:T(8,128)S(1)}, f32[88,512]{1,0:T(8,128)S(1)}, u32[]{:S(2)}, u32[]{:S(2)}) collective-permute-start(f32[88,512]{1,0:T(8,128)S(1)} %collective-permute-done.3.refs_1_), channel_id=1, source_target_pairs={{0,2},{1,3},{2,0},{3,1},{4,6},{5,7},{6,4},{7,5},{8,10},{9,11},{10,... | collective-permute-start | bytes 540680 | tf_op jit(solution)/shard_map/ppermute | solution.py:18
  44.8 2.1 %copy-start.13 = (f32[88,512]{1,0:T(8,128)}, f32[88,512]{1,0:T(8,128)S(1)}, u32[]{:S(2)}) copy-start(f32[88,512]{1,0:T(8,128)S(1)} %collective-permute-done.5.refs_3_) | copy-start | bytes 540676
  44.8 2.1 %collective-permute-start.9 = (f32[88,512]{1,0:T(8,128)S(1)}, f32[88,512]{1,0:T(8,128)S(1)}, u32[]{:S(2)}, u32[]{:S(2)}) collective-permute-start(f32[88,512]{1,0:T(8,128)S(1)} %collective-permute-done.5.refs_3_), channel_id=1, source_target_pairs={{0,1},{1,0},{2,3},{3,2},{4,5},{5,4},{6,7},{7,6},{8,9},{9,8},{10,11... | collective-permute-start | bytes 540680 | tf_op jit(solution)/shard_map/ppermute | solution.py:18
  45.8 1.2 %copy-start.7 = (f32[16,64,128]{2,1,0:T(8,128)}, f32[16,64,128]{2,1,0:T(8,128)S(1)}, u32[]{:S(2)}) copy-start(f32[16,64,128]{2,1,0:T(8,128)S(1)} %collective-permute-done.15.refs_15_) | copy-start | bytes 1572868
  45.8 1.4 %copy-start.8 = (f32[16,64,128]{2,1,0:T(8,128)}, f32[16,64,128]{2,1,0:T(8,128)S(1)}, u32[]{:S(2)}) copy-start(f32[16,64,128]{2,1,0:T(8,128)S(1)} %collective-permute-done.12.refs_11_) | copy-start | bytes 1572868
  45.8 2.0 %copy-start.2 = (f32[16,64,256]{2,1,0:T(8,128)}, f32[16,64,256]{2,1,0:T(8,128)S(1)}, u32[]{:S(2)}) copy-start(f32[16,64,256]{2,1,0:T(8,128)S(1)} %collective-permute-done.10.refs_9_) | copy-start | bytes 3145732
  45.8 1.0 copy-start.3
  47.2 0.7 copy-start.14
